TPU v7x, 32 devices: a whole 2x2x4 slice. The times are simulated.
32 devices in a mesh: dp: 16 (over z, y, core), group: 2 (over x).
Axes of the slice: x: 2, y: 2, z: 4, core: 2. Of those that a mesh axis runs over, the one named last changes fastest.
Arguments:
- rewards: float32 [512, 4096], P(('dp', 'group')), may hold values from -6 to 6
- values: float32 [512, 4096], P(('dp', 'group')), may hold values from -6 to 6
- horizon: float32 [512], P(('dp', 'group')), may hold values from 16 to 32768
- lengths: int32 [512], P(('dp', 'group')), may hold values from 1 to 4096
- assignment: int32 [16, 1024], P('dp', 'group'), may hold values from 0 to 1023, as said below
Outputs:
- returns: float32 [512, 4096], P(('dp', 'group'))
- train_adv: float32 [16384, 128], P(('dp', 'group'))
Inputs may be any that keep to these rules, and one draw needn't show every extreme that they name: Each row of assignment names each of the 1024 blocks of its index of dp once; the slots held by one device take at most 512 blocks from the sequences of any one device of its group, and that most is reached in every row.
All inputs are finite; a program needn't handle non-finite values.
Results may differ from a plain program's by a relative error of at most 0.0001.
Values sent between devices are 32-bit elements; how exact they have to be, the bound alone decides.
No kernel may reach another device: no remote copies, remote signals or barrier semaphores. Data moves between devices by JAX's collectives and lax.ppermute only.
A program may use at most 64 MiB of HBM per device.

v0:
```python
import jax
import jax.numpy as jnp
from jax import lax
from jax.sharding import PartitionSpec as P

LEN = 4096
BLK = 128


trace_decay = 0.998
epsilon = 1e-05


def combined_all(part, axis, combine):
    gathered = jax.tree.map(lambda a: lax.all_gather(a, axis), part)

    def take(source):
        return jax.tree.map(lambda a: lax.dynamic_index_in_dim(a, source, 0, False), gathered)

    return lax.fori_loop(
        1, lax.axis_size(axis), lambda source, state: combine(state, take(source)), take(0)
    )


def merge_moments(first, second):
    total = first[0] + second[0]
    safe = jnp.maximum(total, 1.0)
    offset = second[1] - first[1]
    center = first[1] + offset * second[0] / safe
    spread = first[2] + second[2] + offset * offset * first[0] * second[0] / safe
    return (total, center, spread)


def blocked_discount(deltas, coeff, per_row, width):
    seqs = deltas.shape[0]
    log_rate = jnp.log(coeff)
    stacked = deltas.reshape(seqs, per_row, width)
    inner = jnp.arange(width, dtype=jnp.int32)
    gap = (inner[None, :] - inner[:, None]).astype(jnp.float32)
    within = jnp.where(
        gap[None, :, :] >= 0.0,
        jnp.exp(jnp.maximum(gap, 0.0)[None, :, :] * log_rate[:, None, None]),
        0.0,
    )
    partial_sums = jnp.einsum("sbj,sij->sbi", stacked, within, precision=lax.Precision.HIGHEST)
    block_sums = partial_sums[:, :, 0]
    outer = jnp.arange(per_row, dtype=jnp.int32)
    step_gap = (outer[None, :] - outer[:, None]).astype(jnp.float32)
    across = jnp.where(
        step_gap[None, :, :] >= 0.0,
        jnp.exp(jnp.maximum(step_gap, 0.0)[None, :, :] * (width * log_rate)[:, None, None]),
        0.0,
    )
    starts = jnp.einsum("sc,sbc->sb", block_sums, across, precision=lax.Precision.HIGHEST)
    following = jnp.concatenate([starts[:, 1:], jnp.zeros((seqs, 1), jnp.float32)], axis=1)
    tail_power = jnp.exp((width - inner).astype(jnp.float32)[None, :] * log_rate[:, None])
    total = partial_sums + following[:, :, None] * tail_power[:, None, :]
    return total.reshape(seqs, per_row * width)


def body(rewards, values, horizon, lengths, assignment):
    seqs, local = rewards.shape
    position = jnp.arange(local, dtype=jnp.int32)
    inside = position[None, :] < lengths[:, None]
    follows = position[None, :] + 1 < lengths[:, None]
    shifted = jnp.concatenate([values[:, 1:], jnp.zeros((seqs, 1), jnp.float32)], axis=1)
    upcoming = jnp.where(follows, shifted, 0.0)
    discount = 1.0 - 1.0 / horizon
    deltas = jnp.where(inside, rewards + discount[:, None] * upcoming - values, 0.0)
    per_row = LEN // BLK
    advantage = blocked_discount(deltas, discount * trace_decay, per_row, BLK)
    returns = jnp.where(inside, advantage + values, 0.0)
    weight = inside.astype(jnp.float32)
    counted = jnp.sum(weight)
    center = jnp.sum(advantage * weight) / jnp.maximum(counted, 1.0)
    spread = jnp.sum(weight * (advantage - center) ** 2)
    moments = (counted, center, spread)
    moments = combined_all(moments, "group", merge_moments)
    moments = combined_all(moments, "dp", merge_moments)
    total, middle, deviation = moments
    scale = lax.rsqrt(deviation / total + epsilon)
    slots = assignment.shape[-1]
    wanted = assignment.reshape(slots)
    whitened = jnp.where(inside, (advantage - middle) * scale, 0.0)
    blocks = whitened.reshape(seqs, per_row, BLK)
    piece = lax.all_gather(blocks, "group", axis=0, tiled=True)
    labels = (
        jnp.arange(piece.shape[0], dtype=jnp.int32)[:, None] * per_row
        + jnp.arange(per_row, dtype=jnp.int32)[None, :]
    )
    onehot = (wanted[:, None] == labels.reshape(1, -1)).astype(jnp.float32)
    flat = piece.reshape(piece.shape[0] * per_row, BLK)
    train = jnp.dot(
        onehot, flat, precision=lax.Precision.HIGHEST, preferred_element_type=jnp.float32
    )
    return (returns, train)


def solution(mesh):
    in_specs = (
        P(("dp", "group"), None),
        P(("dp", "group"), None),
        P(("dp", "group")),
        P(("dp", "group")),
        P("dp", "group"),
    )
    out_specs = (P(("dp", "group"), None), P(("dp", "group"), None))
    return jax.shard_map(body, mesh=mesh, in_specs=in_specs, out_specs=out_specs, check_vma=False)
```

profile of v0, /device:TPU:0, one launch (start us, length us, event | category | flops | bytes accessed | tf_op | source)
XLA Modules:
  0.0 144.9 jit_solution(13096418184719665145)
XLA Ops:
  0.7 1.3 dynamic-slice.1
  2.0 1.3 dynamic-slice
  3.3 0.7 broadcast_multiply_fusion
  4.3 1.1 slice.18
  5.6 1.8 %fusion.3 = f32[16,32,128]{2,1,0:T(8,128)S(1)} fusion(f32[16,32,128]{2,1,0:T(8,128)S(1)} %bitcast.48, f32[16]{0:T(128)S(1)} %multiply_log_fusion, f32[128,128]{1,0:T(8,128)S(1)} %convert_maximum_fusion, pred[128,128]{1,0:T(8,128)(4,1)S(1)} %convert_compare_fusion), kind=kOutput, calls=%fused_computation.3 | convolution fusion | flops 101187584 | bytes 606272 | tf_op jit(solution)/shard_map/sbj,sij->sbi/dot_general | solution.py:45
  8.2 0.8 fusion.12
  9.0 1.5 %convert_reduce_fusion = (f32[]{:T(128)}, f32[16,4096]{1,0:T(8,128)}) fusion(s32[16]{0:T(128)S(1)} %copy-done.2, f32[16,4096]{1,0:T(8,128)S(1)} %copy-done, f32[2,8,32,128]{3,2,1,0:T(8,128)S(1)} %bitcast.46), kind=kLoop, calls=%fused_computation.20 | loop fusion | flops 327679 | bytes 786500 | tf_op jit(solution)/shard_map/reduce_sum | solution.py:74
  11.8 0.8 fusion.13
  12.6 0.7 dynamic-update-slice.2
  13.3 1.3 dynamic-update-slice.4
  14.7 1.4 dynamic-update-slice
  16.0 5.8 %all-reduce.9 = (f32[2]{0:T(128)S(1)}, f32[2]{0:T(128)S(1)}, f32[2]{0:T(128)S(1)}) all-reduce(f32[2]{0:T(128)S(1)} %dynamic-update-slice, f32[2]{0:T(128)S(1)} %dynamic-update-slice.2, f32[2]{0:T(128)S(1)} %dynamic-update-slice.4), channel_id=1, replica_groups=mesh['dp'=16,'group'=2] {'group'}, use_global_device_ids=true, to_apply=%add.2 | all-reduce | flops 6 | bytes 48
  23.8 0.7 dynamic-update-slice.1
  24.4 0.6 fusion.25
  30.1 0.7 dynamic-update-slice.5
  30.8 0.7 dynamic-update-slice.3
  31.5 32.8 %all-reduce.8 = (f32[16]{0:T(128)S(1)}, f32[16]{0:T(128)S(1)}, f32[16]{0:T(128)S(1)}) all-reduce(f32[16]{0:T(128)S(1)} %dynamic-update-slice.1, f32[16]{0:T(128)S(1)} %dynamic-update-slice.3, f32[16]{0:T(128)S(1)} %dynamic-update-slice.5), channel_id=1, replica_groups=mesh['dp'=16,'group'=2] {'dp'}, use_global_device_ids=true, to_apply=%add.3 | all-reduce | flops 48 | bytes 384
  64.4 71.4 %while.12 = (s32[]{:T(128)}, f32[]{:T(128)}, f32[]{:T(128)}, f32[]{:T(128)}, f32[16]{0:T(128)S(1)}, /*index=5*/f32[16]{0:T(128)S(1)}, f32[16]{0:T(128)S(1)}, s32[]{:T(128)}, s32[]{:T(128)}, s32[]{:T(128)}, /*index=10*/f32[]{:T(128)}) while((s32[]{:T(128)}, f32[]{:T(128)}, f32[]{:T(128)}, f32[]{:T(128)}, f32[16]{0:T(128)S(1)}, ...), condition=%wide.region_4.5_spmd, body=%wide.region_3.4_spmd.sunk | while | flops 17 | bytes 331 | solution.py:20
  65.6 0.6 dynamic_slice.81
  70.4 0.6 dynamic_slice.81
  75.1 0.6 dynamic_slice.81
  79.9 0.6 dynamic_slice.81
  84.6 0.6 dynamic_slice.81
  89.4 0.6 dynamic_slice.81
  94.2 0.6 dynamic_slice.81
  103.7 0.6 dynamic_slice.81
  108.5 0.6 dynamic_slice.81
  118.0 0.6 dynamic_slice.81
  122.7 0.6 dynamic_slice.81
  132.3 0.6 dynamic_slice.81
  136.0 7.0 %all_gather.51 = f32[32,32,128]{2,1,0:T(8,128)S(1)} all-gather(f32[16,32,128]{2,1,0:T(8,128)S(1)} %compare_select_fusion), channel_id=1, replica_groups=mesh['dp'=16,'group'=2] {'group'}, dimensions={0}, use_global_device_ids=true | all-gather | bytes 786432 | tf_op jit(solution)/shard_map/all_gather | solution.py:86
  143.1 1.8 %fusion = f32[512,128]{1,0:T(8,128)} fusion(f32[1024,128]{1,0:T(8,128)S(1)} %bitcast.47, s32[1024]{0:T(1024)S(1)} %add.168, s32[512]{0:T(512)S(1)} %bitcast.51), kind=kOutput, calls=%fused_computation | convolution fusion | flops 805830656 | bytes 792576 | tf_op jit(solution)/shard_map/dot_general | solution.py:93
  (67 shorter events, 21.3 us)
Async XLA Ops:
  0.6 4.7 %copy-start.2 = (s32[16]{0:T(128)S(1)}, s32[16]{0:T(128)}, u32[]{:S(2)}) copy-start(s32[16]{0:T(128)} %param.10) | copy-start | bytes 196
  0.6 4.7 %copy-start = (f32[16,4096]{1,0:T(8,128)S(1)}, f32[16,4096]{1,0:T(8,128)}, u32[]{:S(2)}) copy-start(f32[16,4096]{1,0:T(8,128)} %param.8) | copy-start | bytes 786436
  0.7 4.7 %copy-start.1 = (f32[16,4096]{1,0:T(8,128)S(1)}, f32[16,4096]{1,0:T(8,128)}, u32[]{:S(2)}) copy-start(f32[16,4096]{1,0:T(8,128)} %param.7) | copy-start | bytes 786436
  136.0 7.1 %copy-start.3 = (s32[1,512]{1,0:T(1,128)S(1)}, s32[1,512]{1,0:T(1,128)}, u32[]{:S(2)}) copy-start(s32[1,512]{1,0:T(1,128)} %param.11) | copy-start | bytes 6148
where the time goes:
time: 146 us; the launch traced here: 145 us
  blocking collectives  45.7 us (31%)
  loops' own time  44.7 us (31%)
  local copies, waits for them, and re-layouts  37.5 us (26%)
  between operations  8.62 us (6%)
  matrix products  4.18 us (3%)
  other arithmetic  4.16 us (3%)
    another operation x1, loops' own time, combined_all(): lax.fori_loop(1, lax.axis_size(axis), lambda source, state: combine(state...  44.7 us
    unnamed x2, blocking collectives  38.7 us
    dynamic_slice x47, local copies, waits for them, and re-layouts, take(): lax.dynamic_index_in_dim(a, source, 0, False)  28 us
    unnamed x23, local copies, waits for them, and re-layouts  8.14 us
    all_gather x1, blocking collectives, body(): piece = lax.all_gather(blocks, 'group', axis=0, tiled=True)  7.04 us

commit v1 on v0

v1 whole, which is shorter than its diff:
```python
import functools

import jax
import jax.numpy as jnp
from jax import lax
from jax.experimental import pallas as pl
from jax.experimental.pallas import tpu as pltpu
from jax.sharding import PartitionSpec as P

BLK = 128
trace_decay = 0.998
epsilon = 1e-05
OUTSIDE = 1e30
LANES = 128
ROWS = 8


def column(ref, first, dtype):
    row = lax.broadcasted_iota(jnp.int32, (ROWS, LANES), 0)
    out = jnp.zeros((ROWS, LANES), dtype)
    for k in range(ROWS):
        out = jnp.where(row == k, ref[first + k], out)
    return out[:, :1]


def advantage_kernel(me_ref, horizon_ref, lengths_ref, rewards_ref, values_ref, returns_ref, blocks_ref, stats_ref):
    seqs, local = rewards_ref.shape
    per_row = local // BLK
    position = lax.broadcasted_iota(jnp.int32, (ROWS, local), 1)
    parts = []
    for first in range(0, seqs, ROWS):
        rows = pl.ds(first, ROWS)
        length = column(lengths_ref, first, jnp.int32)
        discount = 1.0 - 1.0 / column(horizon_ref, first, jnp.float32)
        rewards = rewards_ref[rows, :]
        values = values_ref[rows, :]
        inside = position < length
        shifted = pltpu.roll(values, local - 1, 1)
        upcoming = jnp.where(position + 1 < length, shifted, 0.0)
        total = jnp.where(inside, rewards + discount * upcoming - values, 0.0)
        power = discount * trace_decay
        step = 1
        while step < local:
            ahead = pltpu.roll(total, local - step, 1)
            total = total + power * jnp.where(position < local - step, ahead, 0.0)
            power = power * power
            step *= 2
        returns_ref[rows, :] = jnp.where(inside, total + values, 0.0)
        marked = jnp.where(inside, total, OUTSIDE)
        for block in range(per_row):
            blocks_ref[pl.ds(first * per_row + block, ROWS, stride=per_row), :] = marked[:, block * BLK : (block + 1) * BLK]
        parts.append((inside, total, jnp.sum(length.astype(jnp.float32))))
    count = sum(part[2] for part in parts)
    mean = sum(jnp.sum(part[1]) for part in parts) / count
    spread = sum(jnp.sum(jnp.where(part[0], (part[1] - mean) ** 2, 0.0)) for part in parts)
    wide = stats_ref.shape[1]
    row = lax.broadcasted_iota(jnp.int32, (ROWS, wide), 0)
    mine = lax.broadcasted_iota(jnp.int32, (ROWS, wide), 1) == me_ref[0]
    stats = jnp.where(row == 0, count, jnp.where(row == 1, mean, jnp.where(row == 2, spread, 0.0)))
    stats_ref[...] = jnp.where(mine, stats, 0.0)


def place_kernel(members, me_ref, wanted_ref, stats_ref, *refs):
    sources, (out_ref, pool_ref) = refs[:members], refs[members:]
    slots = out_ref.shape[0]
    share = sources[0].shape[0]
    group = me_ref[1]
    for k in range(members):
        owner = lax.rem(group + k, members)
        pool_ref[pl.ds(pl.multiple_of(owner * share, share), share), :] = sources[k][...]

    def move(i, carry):
        for k in range(ROWS):
            slot = i * ROWS + k
            out_ref[pl.ds(slot, 1), :] = pool_ref[pl.ds(wanted_ref[0, slot], 1), :]
        return carry

    lax.fori_loop(0, slots // ROWS, move, 0)
    count, mean, spread = stats_ref[0:1, :], stats_ref[1:2, :], stats_ref[2:3, :]
    total = jnp.sum(count)
    center = jnp.sum(count * mean) / total
    deviation = jnp.sum(spread + count * (mean - center) ** 2)
    scale = lax.rsqrt(jnp.full((1, LANES), deviation / total + epsilon, jnp.float32))
    moved = out_ref[...]
    out_ref[...] = jnp.where(moved == OUTSIDE, 0.0, (moved - center) * scale)


def merged(mine, other):
    return jnp.where(other[:1] > 0.0, other, mine)


def spread_all(stats, axis, size):
    reach = 1
    while reach < size:
        pairs = [(i, (i + reach) % size) for i in range(size)]
        stats = merged(stats, lax.ppermute(stats, axis, pairs))
        reach *= 2
    return stats


def body(rewards, values, horizon, lengths, assignment):
    seqs, local = rewards.shape
    n_dp, n_group = lax.axis_size("dp"), lax.axis_size("group")
    slots = assignment.shape[-1]
    wide = -(-n_dp * n_group // LANES) * LANES
    group = lax.axis_index("group")
    me = jnp.stack([lax.axis_index("dp") * n_group + group, group]).astype(jnp.int32)
    smem = pl.BlockSpec(memory_space=pltpu.SMEM)
    vmem = pl.BlockSpec(memory_space=pltpu.VMEM)
    f32 = jnp.float32
    returns, blocks, stats = pl.pallas_call(
        advantage_kernel,
        out_shape=(
            jax.ShapeDtypeStruct((seqs, local), f32),
            jax.ShapeDtypeStruct((seqs * local // BLK, BLK), f32),
            jax.ShapeDtypeStruct((ROWS, wide), f32),
        ),
        in_specs=[smem, smem, smem, vmem, vmem],
        out_specs=(vmem, vmem, vmem),
        compiler_params=pltpu.CompilerParams(vmem_limit_bytes=16 << 20),
    )(me, horizon, lengths, rewards, values)
    sources = [blocks]
    for k in range(1, n_group):
        sources.append(lax.ppermute(blocks, "group", [((i + k) % n_group, i) for i in range(n_group)]))
    stats = spread_all(stats, "group", n_group)
    stats = spread_all(stats, "dp", n_dp)
    train = pl.pallas_call(
        functools.partial(place_kernel, n_group),
        out_shape=jax.ShapeDtypeStruct((slots, BLK), f32),
        in_specs=[smem, smem, vmem] + [vmem] * n_group,
        out_specs=vmem,
        scratch_shapes=[pltpu.VMEM((n_group * blocks.shape[0], BLK), f32)],
        compiler_params=pltpu.CompilerParams(vmem_limit_bytes=16 << 20),
    )(me, assignment, stats, *sources)
    return (returns, train)


def solution(mesh):
    in_specs = (
        P(("dp", "group"), None),
        P(("dp", "group"), None),
        P(("dp", "group")),
        P(("dp", "group")),
        P("dp", "group"),
    )
    out_specs = (P(("dp", "group"), None), P(("dp", "group"), None))
    return jax.shard_map(body, mesh=mesh, in_specs=in_specs, out_specs=out_specs, check_vma=False)
```

time: 146 us -> 36.7 us (0.25)
  blocking collectives: 45.7 us -> 0 us
  loops' own time: 44.7 us -> 0 us
  local copies, waits for them, and re-layouts: 37.5 us -> 2.48 us
  waiting for transfers between devices: 0 us -> 23.3 us
  between operations: 8.62 us -> 0.7 us
  starting transfers between devices: 0 us -> 5.29 us
  Pallas kernels: 0 us -> 4.55 us
  matrix products: 4.18 us -> 0 us
  other arithmetic: 4.16 us -> 0.14 us
    another operation x1 -> x0, loops' own time: 44.7 us -> none  [combined_all(): lax.fori_loop(1, lax.axis_size(axis), lambda source, state: combine(state...]
    unnamed x2 -> x0, blocking collectives: 38.7 us -> none
    dynamic_slice x47 -> x0, local copies, waits for them, and re-layouts: 28 us -> none  [take(): lax.dynamic_index_in_dim(a, source, 0, False)]
    ppermute x0 -> x6, waiting for transfers between devices: none -> 23.3 us  [the longest x5 21.4 us: spread_all(): stats = merged(stats, lax.ppermute(stats, axis, pairs))]
    all_gather x1 -> x0, blocking collectives: 7.04 us -> none  [body(): piece = lax.all_gather(blocks, 'group', axis=0, tiled=True)]
    unnamed x23 -> x10, local copies, waits for them, and re-layouts: 8.14 us -> 2.48 us
    ppermute x0 -> x6, starting transfers between devices: none -> 5.29 us  [the longest x5 3.21 us: spread_all(): stats = merged(stats, lax.ppermute(stats, axis, pairs))]
    pallas_call x0 -> x2, Pallas kernels: none -> 4.55 us  [the longest x1 2.32 us: body(): pl.pallas_call(functools.partial(place_kernel, n_group), out_shape=jax.Sh...]
  transfers between devices with their start and end apart: 0 -> 6, of which waited for: 0 -> 6; matrix products, arithmetic and copies ran while one was open for 0% -> 0% of each run, Pallas kernels for 0% -> 0%
where the time goes in v1:
time: 36.7 us; the launch traced here: 36.5 us
  waiting for transfers between devices  23.3 us (63%)
  starting transfers between devices  5.29 us (14%)
  Pallas kernels  4.55 us (12%)
  local copies, waits for them, and re-layouts  2.48 us (7%)
  between operations  0.7 us (2%)
    ppermute x5, waiting for transfers between devices, spread_all(): stats = merged(stats, lax.ppermute(stats, axis, pairs))  21.4 us
    ppermute x5, starting transfers between devices, spread_all(): stats = merged(stats, lax.ppermute(stats, axis, pairs))  3.21 us
    unnamed x10, local copies, waits for them, and re-layouts  2.48 us
    pallas_call x1, Pallas kernels, body(): pl.pallas_call(functools.partial(place_kernel, n_group), out_shape=jax.Sh...  2.32 us
    pallas_call x1, Pallas kernels, body(): pl.pallas_call(advantage_kernel, out_shape=(jax.ShapeDtypeStruct((seqs, l...  2.23 us
    ppermute x1, starting transfers between devices, body(): lax.ppermute(blocks, 'group', [((i + k) % n_group, i) for i in range(n_gr...  2.09 us
    ppermute x1, waiting for transfers between devices, body(): lax.ppermute(blocks, 'group', [((i + k) % n_group, i) for i in range(n_gr...  1.93 us
  transfers between devices with their start and end apart: 6, of which 6 were waited for; matrix products, arithmetic and copies ran while one was open for 0% of the time, Pallas kernels for 0%

profile of v1, /device:TPU:0, one launch (start us, length us, event | category | flops | bytes accessed | tf_op | source)
XLA Modules:
  0.0 36.5 jit_solution(4693330644177938438)
XLA Ops:
  0.6 0.0 copy-start.3
  0.6 0.0 copy-start.4
  0.7 0.1 pad_add_fusion.me_ref
  0.7 0.6 %copy-done.3 = f32[16]{0:T(128)S(1)} copy-done((f32[16]{0:T(128)S(1)}, f32[16]{0:T(128)}, u32[]{:S(2)}) %copy-start.3) | copy-done | bytes 88
  1.3 0.0 copy-done.4
  1.3 0.0 copy-start
  1.3 0.9 %copy-done = f32[16,4096]{1,0:T(8,128)S(1)} copy-done((f32[16,4096]{1,0:T(8,128)S(1)}, f32[16,4096]{1,0:T(8,128)}, u32[]{:S(2)}) %copy-start) | copy-done | bytes 262168
  2.3 0.0 copy-start.1
  2.3 0.9 %copy-done.1 = f32[16,4096]{1,0:T(8,128)S(1)} copy-done((f32[16,4096]{1,0:T(8,128)S(1)}, f32[16,4096]{1,0:T(8,128)}, u32[]{:S(2)}) %copy-start.1) | copy-done | bytes 262168
  3.2 2.2 %shard_map.68 = (f32[16,4096]{1,0:T(8,128)}, f32[512,128]{1,0:T(8,128)S(1)}, f32[8,128]{1,0:T(8,128)S(1)}) custom-call(s32[2]{0:T(128)S(1)} %pad_add_fusion.me_ref, f32[16]{0:T(128)S(1)} %copy-done.3, s32[16]{0:T(128)S(1)} %copy-done.4, f32[16,4096]{1,0:T(8,128)S(1)} %copy-done, f32[16,4096]{1,0:T(8,128)S(1)} %copy-done.1), custom_call_target="tpu_custom_call" | custom-call | tf_op jit(solution)/shard_map/pallas_call | solution.py:111
  5.4 3.0 %collective-permute-start = (f32[8,128]{1,0:T(8,128)S(1)}, f32[8,128]{1,0:T(8,128)S(1)}, u32[]{:S(2)}, u32[]{:S(2)}) collective-permute-start(f32[8,128]{1,0:T(8,128)S(1)} %get-tuple-element.6), channel_id=1, source_target_pairs={{0,1},{1,0},{2,3},{3,2},{4,5},{5,4},{6,7},{7,6},{8,9},{9,8},{10,11... | collective-permute-start | bytes 12296 | tf_op jit(solution)/shard_map/ppermute | solution.py:96
  8.4 1.6 %collective-permute-done = f32[8,128]{1,0:T(8,128)S(1)} collective-permute-done((f32[8,128]{1,0:T(8,128)S(1)}, f32[8,128]{1,0:T(8,128)S(1)}, u32[]{:S(2)}, u32[]{:S(2)}) %collective-permute-start) | collective-permute-done | bytes 4128 | tf_op jit(solution)/shard_map/ppermute | solution.py:96
  10.0 0.1 collective-permute-start.1
  10.1 5.7 %collective-permute-done.1 = f32[8,128]{1,0:T(8,128)S(1)} collective-permute-done((f32[8,128]{1,0:T(8,128)S(1)}, f32[8,128]{1,0:T(8,128)S(1)}, u32[]{:S(2)}, u32[]{:S(2)}) %collective-permute-start.1) | collective-permute-done | bytes 4128 | tf_op jit(solution)/shard_map/ppermute | solution.py:96
  15.8 0.1 collective-permute-start.2
  15.9 6.3 %collective-permute-done.2 = f32[8,128]{1,0:T(8,128)S(1)} collective-permute-done((f32[8,128]{1,0:T(8,128)S(1)}, f32[8,128]{1,0:T(8,128)S(1)}, u32[]{:S(2)}, u32[]{:S(2)}) %collective-permute-start.2) | collective-permute-done | bytes 4128 | tf_op jit(solution)/shard_map/ppermute | solution.py:96
  22.2 0.1 collective-permute-start.3
  22.2 5.4 %collective-permute-done.3 = f32[8,128]{1,0:T(8,128)S(1)} collective-permute-done((f32[8,128]{1,0:T(8,128)S(1)}, f32[8,128]{1,0:T(8,128)S(1)}, u32[]{:S(2)}, u32[]{:S(2)}) %collective-permute-start.3) | collective-permute-done | bytes 4128 | tf_op jit(solution)/shard_map/ppermute | solution.py:96
  27.6 0.1 collective-permute-start.4
  27.7 2.1 %collective-permute-start.5 = (f32[512,128]{1,0:T(8,128)S(1)}, f32[512,128]{1,0:T(8,128)S(1)}, u32[]{:S(2)}, u32[]{:S(2)}) collective-permute-start(f32[512,128]{1,0:T(8,128)S(1)} %get-tuple-element.7.refs_0_), channel_id=1, source_target_pairs={{1,0},{0,1},{3,2},{2,3},{5,4},{4,5},{7,6},{6,7},{9,8},{8,9},{11,10... | collective-permute-start | bytes 786440 | tf_op jit(solution)/shard_map/ppermute | solution.py:124
  29.8 2.4 %collective-permute-done.4 = f32[8,128]{1,0:T(8,128)S(1)} collective-permute-done((f32[8,128]{1,0:T(8,128)S(1)}, f32[8,128]{1,0:T(8,128)S(1)}, u32[]{:S(2)}, u32[]{:S(2)}) %collective-permute-start.4) | collective-permute-done | bytes 4128 | tf_op jit(solution)/shard_map/ppermute | solution.py:96
  32.2 0.0 copy-start.2
  32.2 1.9 %collective-permute-done.5.refs_1_ = f32[512,128]{1,0:T(8,128)S(1)} collective-permute-done((f32[512,128]{1,0:T(8,128)S(1)}, f32[512,128]{1,0:T(8,128)S(1)}, u32[]{:S(2)}, u32[]{:S(2)}) %collective-permute-start.5) | collective-permute-done | bytes 262176 | tf_op jit(solution)/shard_map/ppermute | solution.py:124
  34.2 0.0 copy-done.2
  34.2 2.3 %shard_map.69 = f32[512,128]{1,0:T(8,128)} custom-call(s32[2]{0:T(128)S(1)} %pad_add_fusion.me_ref, s32[1,512]{1,0:T(1,128)S(1)} %copy-done.2, f32[8,128]{1,0:T(8,128)S(1)} %broadcast_select_fusion.stats_ref, f32[512,128]{1,0:T(8,128)S(1)} %get-tuple-element.7.refs_0_, f32[512,128]{1,0:T(8,128)S(1)} %collective-permute-done.5.refs_1_), custom_call_target="tpu_custom_call" | custom-call | tf_op jit(solution)/shard_map/pallas_call | solution.py:127
  (10 shorter events, 0.1 us)
Async XLA Ops:
  0.6 0.7 %copy-start.3 = (f32[16]{0:T(128)S(1)}, f32[16]{0:T(128)}, u32[]{:S(2)}) copy-start(f32[16]{0:T(128)} %horizon_ref.1) | copy-start | bytes 196
  0.6 0.7 %copy-start.4 = (s32[16]{0:T(128)S(1)}, s32[16]{0:T(128)}, u32[]{:S(2)}) copy-start(s32[16]{0:T(128)} %lengths_ref.1) | copy-start | bytes 196
  1.3 0.9 %copy-start = (f32[16,4096]{1,0:T(8,128)S(1)}, f32[16,4096]{1,0:T(8,128)}, u32[]{:S(2)}) copy-start(f32[16,4096]{1,0:T(8,128)} %rewards_ref.1) | copy-start | bytes 786436
  2.3 0.9 %copy-start.1 = (f32[16,4096]{1,0:T(8,128)S(1)}, f32[16,4096]{1,0:T(8,128)}, u32[]{:S(2)}) copy-start(f32[16,4096]{1,0:T(8,128)} %values_ref.1) | copy-start | bytes 786436
  5.4 4.6 %collective-permute-start = (f32[8,128]{1,0:T(8,128)S(1)}, f32[8,128]{1,0:T(8,128)S(1)}, u32[]{:S(2)}, u32[]{:S(2)}) collective-permute-start(f32[8,128]{1,0:T(8,128)S(1)} %get-tuple-element.6), channel_id=1, source_target_pairs={{0,1},{1,0},{2,3},{3,2},{4,5},{5,4},{6,7},{7,6},{8,9},{9,8},{10,11... | collective-permute-start | bytes 12296 | tf_op jit(solution)/shard_map/ppermute | solution.py:96
  10.0 5.8 %collective-permute-start.1 = (f32[8,128]{1,0:T(8,128)S(1)}, f32[8,128]{1,0:T(8,128)S(1)}, u32[]{:S(2)}, u32[]{:S(2)}) collective-permute-start(f32[8,128]{1,0:T(8,128)S(1)} %broadcast_select_fusion.4), channel_id=1, source_target_pairs={{0,2},{2,4},{4,6},{6,8},{8,10},{10,12},{12,14},{14,16},{16,18},{18... | collective-permute-start | bytes 12296 | tf_op jit(solution)/shard_map/ppermute | solution.py:96
  15.8 6.4 %collective-permute-start.2 = (f32[8,128]{1,0:T(8,128)S(1)}, f32[8,128]{1,0:T(8,128)S(1)}, u32[]{:S(2)}, u32[]{:S(2)}) collective-permute-start(f32[8,128]{1,0:T(8,128)S(1)} %broadcast_select_fusion.3), channel_id=1, source_target_pairs={{0,4},{2,6},{4,8},{6,10},{8,12},{10,14},{12,16},{14,18},{16,20},{1... | collective-permute-start | bytes 12296 | tf_op jit(solution)/shard_map/ppermute | solution.py:96
  22.2 5.5 %collective-permute-start.3 = (f32[8,128]{1,0:T(8,128)S(1)}, f32[8,128]{1,0:T(8,128)S(1)}, u32[]{:S(2)}, u32[]{:S(2)}) collective-permute-start(f32[8,128]{1,0:T(8,128)S(1)} %broadcast_select_fusion.2), channel_id=1, source_target_pairs={{0,8},{2,10},{4,12},{6,14},{8,16},{10,18},{12,20},{14,22},{16,24},... | collective-permute-start | bytes 12296 | tf_op jit(solution)/shard_map/ppermute | solution.py:96
  27.6 4.6 %collective-permute-start.4 = (f32[8,128]{1,0:T(8,128)S(1)}, f32[8,128]{1,0:T(8,128)S(1)}, u32[]{:S(2)}, u32[]{:S(2)}) collective-permute-start(f32[8,128]{1,0:T(8,128)S(1)} %broadcast_select_fusion.1), channel_id=1, source_target_pairs={{0,16},{2,18},{4,20},{6,22},{8,24},{10,26},{12,28},{14,30},{16,0},... | collective-permute-start | bytes 12296 | tf_op jit(solution)/shard_map/ppermute | solution.py:96
  27.7 6.4 %collective-permute-start.5 = (f32[512,128]{1,0:T(8,128)S(1)}, f32[512,128]{1,0:T(8,128)S(1)}, u32[]{:S(2)}, u32[]{:S(2)}) collective-permute-start(f32[512,128]{1,0:T(8,128)S(1)} %get-tuple-element.7.refs_0_), channel_id=1, source_target_pairs={{1,0},{0,1},{3,2},{2,3},{5,4},{4,5},{7,6},{6,7},{9,8},{8,9},{11,10... | collective-permute-start | bytes 786440 | tf_op jit(solution)/shard_map/ppermute | solution.py:124
  32.2 1.9 %copy-start.2 = (s32[1,512]{1,0:T(1,128)S(1)}, s32[1,512]{1,0:T(1,128)}, u32[]{:S(2)}) copy-start(s32[1,512]{1,0:T(1,128)} %wanted_ref.1) | copy-start | bytes 6148
